TPU v7x, 32 devices: a whole 2x2x4 slice. The times are simulated.
32 devices in a mesh: parts: 2 (over x), rows: 16 (over z, y, core).
Axes of the slice: x: 2, y: 2, z: 4, core: 2. Of those that a mesh axis runs over, the one named last changes fastest.
Arguments:
- pair: bfloat16 [64, 32, 128], P(('parts', 'rows')), parts along dimension 0, may hold values from -16 to 16
- mask: int32 [64], P('parts'), parts along dimension 0, may hold values from 0 to 1, as said below
- w_tri_in: bfloat16 [128, 512], replicated, may hold values from -0.5 to 0.5
- w_tri_gate: bfloat16 [128, 128], replicated, may hold values from -0.5 to 0.5
- w_tri_out: bfloat16 [128, 128], replicated, may hold values from -0.5 to 0.5
- w_qkv: bfloat16 [128, 384], replicated, may hold values from -0.5 to 0.5
- w_att_bias: bfloat16 [128, 4], replicated, may hold values from -80 to 80
- w_att_gate: bfloat16 [128, 128], replicated, may hold values from -0.5 to 0.5
- w_att_out: bfloat16 [128, 128], replicated, may hold values from -0.5 to 0.5
Outputs:
- updated: bfloat16 [64, 32, 128], P(('parts', 'rows')), parts along dimension 0
There are 2 independent parts, one for each index of `parts`. A program takes and returns all parts, laid end to end along the dimension named above; an argument that names none is the same for every part. Nothing has to cross between parts.
Inputs may be any that keep to these rules, and one draw needn't show every extreme that they name: `mask`: 0 on every residue from some L on, with 16 <= L <= 31; before L each residue may be 1 or 0 (unresolved); residue 0 is always 1.
All inputs are finite; a program needn't handle non-finite values.
Results may differ from a plain program's by a relative error of at most 0.012.
Values may be sent and summed in bfloat16 or wider, within the bound.
A program may use at most 64 MiB of HBM per device.

v0:
```python
import jax
import jax.numpy as jnp
from jax import lax
from jax.sharding import PartitionSpec as P

HEADS = 4
HEAD_DIM = 32


EPSILON = 1e-05
MASK_PENALTY = 1000000000.0


def normalize(values, along_axis):
    values = values.astype(jnp.float32)
    center = jnp.mean(values, axis=along_axis, keepdims=True)
    shifted = values - center
    spread = jnp.mean(shifted * shifted, axis=along_axis, keepdims=True)
    return shifted * lax.rsqrt(spread + EPSILON)


def attend(queries, key_rows, values, score_bias, key_penalty, score_scale):
    column_count = queries.shape[1]
    heads_here = queries.shape[2]
    block_size = max(1, 4 // heads_here)

    def reorder(tensor):
        return tensor.reshape(
            tensor.shape[0], column_count // block_size, block_size, heads_here, -1
        ).transpose(1, 0, 2, 3, 4)

    def one_block(inputs):
        query_part, key_part, value_part = inputs
        scores = (
            jnp.einsum("kbhd,ibhd->bhki", key_part, query_part, preferred_element_type=jnp.float32)
            * score_scale
        )
        scores = scores + score_bias[None] + key_penalty[None, None, :, None]
        row_peak = jnp.max(scores, axis=2, keepdims=True)
        weights = jnp.exp(scores - row_peak)
        weights = (weights / jnp.sum(weights, axis=2, keepdims=True)).astype(jnp.bfloat16)
        result = jnp.einsum(
            "bhki,kbhd->ibhd", weights, value_part, preferred_element_type=jnp.float32
        )
        return result.astype(jnp.bfloat16)

    outputs = lax.map(one_block, (reorder(queries), reorder(key_rows), reorder(values)))
    return outputs.transpose(1, 0, 2, 3, 4).reshape(queries.shape)


def local(pair, mask, w_tri_in, w_tri_gate, w_tri_out, w_qkv, w_att_bias, w_att_gate, w_att_out):
    row_count = pair.shape[0]
    residues = pair.shape[1]
    devices = lax.axis_size("rows")
    first_row = lax.axis_index("rows") * row_count
    key_mask = mask.astype(jnp.float32)
    row_mask = lax.dynamic_slice_in_dim(key_mask, first_row, row_count, 0)
    key_penalty = (key_mask - 1.0) * MASK_PENALTY
    normed = normalize(pair, 2).astype(jnp.bfloat16)
    projected = jnp.einsum("rkc,cf->frk", normed, w_tri_in, preferred_element_type=jnp.float32)
    hidden = w_tri_out.shape[0]
    pair_mask = row_mask[:, None] * key_mask[None, :]
    left_side = (
        jax.nn.sigmoid(projected[:hidden]) * projected[hidden : 2 * hidden] * pair_mask
    ).astype(jnp.bfloat16)
    right_side = (
        jax.nn.sigmoid(projected[2 * hidden : 3 * hidden]) * projected[3 * hidden :] * pair_mask
    ).astype(jnp.bfloat16)
    left_cols, right_cols = (
        lax.all_to_all(left_side, "rows", split_axis=0, concat_axis=1, tiled=True),
        lax.all_to_all(right_side, "rows", split_axis=0, concat_axis=1, tiled=True),
    )
    product = jnp.einsum(
        "cik,cjk->cij", left_cols, right_cols, preferred_element_type=jnp.float32
    ).astype(jnp.bfloat16)
    triangle_rows = lax.all_to_all(product, "rows", split_axis=1, concat_axis=0, tiled=True)
    triangle_normed = normalize(triangle_rows, 0).astype(jnp.bfloat16)
    triangle_gate = jax.nn.sigmoid(
        jnp.einsum("rjc,cd->rjd", normed, w_tri_gate, preferred_element_type=jnp.float32)
    )
    triangle_update = jnp.einsum(
        "crj,cd->rjd", triangle_normed, w_tri_out, preferred_element_type=jnp.float32
    )
    middle = lax.optimization_barrier(
        (pair.astype(jnp.float32) + triangle_gate * triangle_update).astype(jnp.bfloat16)
    )
    attention_input = normalize(middle, 2).astype(jnp.bfloat16)
    bias_rows = jnp.einsum(
        "kic,ch->hki", attention_input, w_att_bias, preferred_element_type=jnp.float32
    )
    score_scale = HEAD_DIM ** (-0.5)
    groups = devices // HEADS
    group_width = residues // groups
    projections = jnp.einsum(
        "rgwc,cthd->hgrtwd",
        attention_input.reshape(row_count, groups, group_width, -1),
        w_qkv.reshape(-1, 3, HEADS, HEAD_DIM),
        preferred_element_type=jnp.float32,
    ).astype(jnp.bfloat16)
    outgoing = projections.reshape(devices, row_count, 3, group_width * HEAD_DIM)
    received = lax.all_to_all(outgoing, "rows", split_axis=0, concat_axis=1, tiled=True)
    bias_copies = jnp.repeat(bias_rows, groups, axis=0)
    head_bias = lax.all_to_all(bias_copies, "rows", split_axis=0, concat_axis=1, tiled=True)
    pieces = received.reshape(residues, 3, group_width, 1, HEAD_DIM)
    attended = attend(pieces[:, 0], pieces[:, 1], pieces[:, 2], head_bias, key_penalty, score_scale)
    returned = lax.all_to_all(
        attended.reshape(residues, group_width, HEAD_DIM),
        "rows",
        split_axis=0,
        concat_axis=1,
        tiled=True,
    )
    attention_rows = (
        returned.reshape(row_count, HEADS, groups, group_width, HEAD_DIM)
        .transpose(0, 2, 3, 1, 4)
        .reshape(row_count, residues, HEADS * HEAD_DIM)
    )
    attention_gate = jax.nn.sigmoid(
        jnp.einsum("rjc,cf->rjf", attention_input, w_att_gate, preferred_element_type=jnp.float32)
    )
    gated_output = (attention_gate * attention_rows.astype(jnp.float32)).astype(jnp.bfloat16)
    result = middle.astype(jnp.float32) + jnp.einsum(
        "rjf,fc->rjc", gated_output, w_att_out, preferred_element_type=jnp.float32
    )
    return result.astype(jnp.bfloat16)


def solution(mesh):
    placed = (P(("parts", "rows"), None, None), P("parts"), P(), P(), P(), P(), P(), P(), P())
    return jax.shard_map(
        local,
        mesh=mesh,
        in_specs=placed,
        out_specs=P(("parts", "rows"), None, None),
        check_vma=False,
    )
```

profile of v0, /device:TPU:0, one launch (start us, length us, event | category | flops | bytes accessed | tf_op | source)
XLA Modules:
  0.0 73.1 jit_solution(14103554241699838095)
XLA Ops:
  0.0 0.0 copy-start
  0.0 0.7 convert_element_type.92
  0.7 0.1 dynamic_slice.13
  0.8 0.1 broadcast_multiply_fusion
  0.9 0.0 copy-done.1
  0.9 0.1 convert_reduce_fusion.1
  1.0 0.2 fusion.50
  1.1 0.0 copy-done
  1.1 0.2 convolution_bitcast_fusion
  1.3 0.1 fusion.53
  1.4 0.1 copy.52
  1.6 0.7 reshape.158
  2.3 7.4 %all-to-all-start = ((bf16[16,2,256]{2,1,0:T(2,128)(2,1)}), bf16[16,2,256]{2,1,0:T(2,128)(2,1)S(1)}, u32[]{:S(2)}, u32[]{:S(2)}) async-start(bf16[16,2,256]{2,1,0:T(2,128)(2,1)} %reshape.158), calls=%async_computation | async-start | bytes 32768 | tf_op jit(solution)/shard_map/all_to_all | solution.py:70
  9.7 0.1 copy.55
  9.8 0.7 reshape.160
  10.5 5.7 %all-to-all-done = bf16[16,2,256]{2,1,0:T(2,128)(2,1)S(1)} async-done(((bf16[16,2,256]{2,1,0:T(2,128)(2,1)}), bf16[16,2,256]{2,1,0:T(2,128)(2,1)S(1)}, u32[]{:S(2)}, u32[]{:S(2)}) %all-to-all-start) | async-done | bytes 16416 | tf_op jit(solution)/shard_map/all_to_all | solution.py:70
  16.2 3.5 %all-to-all-start.1 = ((bf16[16,2,256]{2,1,0:T(2,128)(2,1)}), bf16[16,2,256]{2,1,0:T(2,128)(2,1)S(1)}, u32[]{:S(2)}, u32[]{:S(2)}) async-start(bf16[16,2,256]{2,1,0:T(2,128)(2,1)} %reshape.160), calls=%async_computation.1 | async-start | bytes 32768 | tf_op jit(solution)/shard_map/all_to_all | solution.py:71
  19.7 0.0 copy-done.3
  19.7 0.2 fusion.32
  19.9 0.1 reshape.159
  20.1 0.1 copy.54
  20.1 6.0 %all-to-all-done.1 = bf16[16,2,256]{2,1,0:T(2,128)(2,1)S(1)} async-done(((bf16[16,2,256]{2,1,0:T(2,128)(2,1)}), bf16[16,2,256]{2,1,0:T(2,128)(2,1)S(1)}, u32[]{:S(2)}, u32[]{:S(2)}) %all-to-all-start.1) | async-done | bytes 16416 | tf_op jit(solution)/shard_map/all_to_all | solution.py:71
  26.2 0.1 reshape.161
  26.3 0.1 copy.57
  26.4 0.2 convolution_convert_fusion.2
  26.5 0.0 copy-start.2
  26.6 0.7 reshape.162
  27.3 3.6 %all-to-all-start.2 = ((bf16[16,2,256]{2,1,0:T(2,128)(2,1)}), bf16[16,2,256]{2,1,0:T(2,128)(2,1)S(1)}, u32[]{:S(2)}, u32[]{:S(2)}) async-start(bf16[16,2,256]{2,1,0:T(2,128)(2,1)} %reshape.162), calls=%async_computation.2 | async-start | bytes 32768 | tf_op jit(solution)/shard_map/all_to_all | solution.py:76
  31.0 0.1 copy.61
  31.1 6.3 %all-to-all-done.2 = bf16[16,2,256]{2,1,0:T(2,128)(2,1)S(1)} async-done(((bf16[16,2,256]{2,1,0:T(2,128)(2,1)}), bf16[16,2,256]{2,1,0:T(2,128)(2,1)S(1)}, u32[]{:S(2)}, u32[]{:S(2)}) %all-to-all-start.2) | async-done | bytes 16416 | tf_op jit(solution)/shard_map/all_to_all | solution.py:76
  37.4 0.1 reshape.163
  37.6 0.7 copy-done.4
  38.3 0.2 fusion.33
  38.5 0.1 convert_reduce_fusion
  38.6 0.2 fusion.48
  38.8 0.3 fusion.24
  39.1 0.8 %reshape.157 = bf16[16,2,3,256]{3,1,2,0:T(2,128)(2,1)} reshape(bf16[4,4,2,3,8,32]{5,4,2,3,1,0:T(8,128)(2,1)S(1)} %copy.75) | data formatting | bytes 98304 | tf_op jit(solution)/shard_map/reshape | solution.py:100
  39.9 3.6 %all-to-all-start.3 = ((bf16[16,2,3,256]{3,1,2,0:T(2,128)(2,1)}), bf16[16,2,3,256]{3,1,2,0:T(2,128)(2,1)S(1)}, u32[]{:S(2)}, u32[]{:S(2)}) async-start(bf16[16,2,3,256]{3,1,2,0:T(2,128)(2,1)} %reshape.157), calls=%async_computation.3 | async-start | bytes 98304 | tf_op jit(solution)/shard_map/all_to_all | solution.py:101
  43.5 0.0 copy-done.7
  43.6 0.2 convolution_bitcast_fusion.1
  43.8 6.5 %all-to-all-done.3 = bf16[16,2,3,256]{3,1,2,0:T(2,128)(2,1)S(1)} async-done(((bf16[16,2,3,256]{3,1,2,0:T(2,128)(2,1)}), bf16[16,2,3,256]{3,1,2,0:T(2,128)(2,1)S(1)}, u32[]{:S(2)}, u32[]{:S(2)}) %all-to-all-start.3) | async-done | bytes 49184 | tf_op jit(solution)/shard_map/all_to_all | solution.py:101
  50.3 0.6 broadcast_in_dim.8
  50.9 3.5 %all-to-all-start.4 = ((f32[16,2,32]{2,1,0:T(2,128)}), f32[16,2,32]{2,1,0:T(2,128)S(1)}, u32[]{:S(2)}, u32[]{:S(2)}) async-start(f32[16,2,32]{2,1,0:T(2,128)} %bitcast.36), calls=%async_computation.4 | async-start | bytes 32768 | tf_op jit(solution)/shard_map/all_to_all | solution.py:103
  54.4 0.2 reshape.141
  54.6 0.1 copy.65
  54.8 6.1 %all-to-all-done.4 = f32[16,2,32]{2,1,0:T(2,128)S(1)} async-done(((f32[16,2,32]{2,1,0:T(2,128)}), f32[16,2,32]{2,1,0:T(2,128)S(1)}, u32[]{:S(2)}, u32[]{:S(2)}) %all-to-all-start.4) | async-done | bytes 4128 | tf_op jit(solution)/shard_map/all_to_all | solution.py:103
  60.9 1.0 %while.10 = (s32[]{:T(128)}, bf16[2,32,4,1,32]{1,4,2,3,0:T(8,128)(2,1)S(1)}, bf16[2,32,4,1,32]{1,4,2,3,0:T(8,128)(2,1)S(1)}, bf16[2,32,4,1,32]{4,1,2,3,0:T(8,128...) while((s32[]{:T(128)}, ...), condition=%wide.region_9.10_spmd, body=%wide.region_6.9_spmd.sunk | while | flops 835776 | bytes 383573 | solution.py:47
  60.9 0.1 fusion.111
  61.0 0.2 fusion.110
  61.2 0.2 fusion.112
  61.4 0.1 fusion.111
  61.5 0.2 fusion.110
  61.7 0.2 fusion.112
  61.8 0.1 copy.69
  62.0 0.1 reshape.164
  62.1 9.1 %all_to_all.78 = bf16[16,2,256]{2,1,0:T(2,128)(2,1)S(1)} all-to-all(bf16[16,2,256]{2,1,0:T(2,128)(2,1)S(1)} %reshape.164), channel_id=1, replica_groups=mesh['parts'=2,'rows'=16] {'rows'}, dimensions={0} | all-to-all | bytes 32768 | tf_op jit(solution)/shard_map/all_to_all | solution.py:106
  71.1 0.1 reshape.165
  71.3 0.1 copy.71
  71.4 0.0 copy-start.5
  71.4 0.0 copy-start.6
  71.4 0.1 reshape.144
  71.5 0.6 copy-done.5
  72.1 0.0 copy-done.6
  72.1 0.9 %fusion.35 = bf16[2,32,128]{2,1,0:T(8,128)(2,1)} fusion(f32[2,32,128]{2,1,0:T(8,128)S(1)} %reshape.144, bf16[2,32,128]{2,1,0:T(8,128)(2,1)S(1)} %fusion.33, bf16[128,128]{1,0:T(8,128)(2,1)S(1)} %copy-done.5, bf16[128,128]{1,0:T(8,128)(2,1)S(1)} %copy-done.6, f32[2,32]{1,0:T(2,128)S(1)} %add_rsqrt_fusion, f32[2,32]{1,0:T(2,128)S(1)} %broadcast_multiply_fusion.1), kind=kOutput, calls=%fused_computation.40 | convolution fusion | flops 4292608 | bytes 131584 | tf_op jit(solution)/shard_map/rjf,fc->rjc/dot_general | solution.py:122
  (27 shorter events, 0.3 us)
Async XLA Ops:
  0.0 1.1 %copy-start = (bf16[128,512]{1,0:T(8,128)(2,1)S(1)}, bf16[128,512]{1,0:T(8,128)(2,1)}, u32[]{:S(2)}) copy-start(bf16[128,512]{1,0:T(8,128)(2,1)} %param.13) | copy-start | bytes 393220
  0.0 0.9 %copy-start.1 = (bf16[2,32,128]{2,1,0:T(8,128)(2,1)S(1)}, bf16[2,32,128]{2,1,0:T(8,128)(2,1)}, u32[]{:S(2)}) copy-start(bf16[2,32,128]{2,1,0:T(8,128)(2,1)} %param.11) | copy-start | bytes 49156
  2.3 13.9 %all-to-all-start = ((bf16[16,2,256]{2,1,0:T(2,128)(2,1)}), bf16[16,2,256]{2,1,0:T(2,128)(2,1)S(1)}, u32[]{:S(2)}, u32[]{:S(2)}) async-start(bf16[16,2,256]{2,1,0:T(2,128)(2,1)} %reshape.158), calls=%async_computation | async-start | bytes 32768 | tf_op jit(solution)/shard_map/all_to_all | solution.py:70
  10.5 9.2 %copy-start.3 = (bf16[128,128]{1,0:T(8,128)(2,1)S(1)}, bf16[128,128]{1,0:T(8,128)(2,1)}, u32[]{:S(2)}) copy-start(bf16[128,128]{1,0:T(8,128)(2,1)} %param.14) | copy-start | bytes 98308
  16.2 10.0 %all-to-all-start.1 = ((bf16[16,2,256]{2,1,0:T(2,128)(2,1)}), bf16[16,2,256]{2,1,0:T(2,128)(2,1)S(1)}, u32[]{:S(2)}, u32[]{:S(2)}) async-start(bf16[16,2,256]{2,1,0:T(2,128)(2,1)} %reshape.160), calls=%async_computation.1 | async-start | bytes 32768 | tf_op jit(solution)/shard_map/all_to_all | solution.py:71
  26.5 4.4 %copy-start.2 = (bf16[128,384]{1,0:T(8,128)(2,1)S(1)}, bf16[128,384]{1,0:T(8,128)(2,1)}, u32[]{:S(2)}) copy-start(bf16[128,384]{1,0:T(8,128)(2,1)} %param.16) | copy-start | bytes 294916
  27.3 3.6 %copy-start.8 = (s32[32]{0:T(128)S(1)}, s32[32]{0:T(128)}, u32[]{:S(2)}) copy-start(s32[32]{0:T(128)} %param.12) | copy-start | bytes 388
  27.3 10.1 %all-to-all-start.2 = ((bf16[16,2,256]{2,1,0:T(2,128)(2,1)}), bf16[16,2,256]{2,1,0:T(2,128)(2,1)S(1)}, u32[]{:S(2)}, u32[]{:S(2)}) async-start(bf16[16,2,256]{2,1,0:T(2,128)(2,1)} %reshape.162), calls=%async_computation.2 | async-start | bytes 32768 | tf_op jit(solution)/shard_map/all_to_all | solution.py:76
  37.6 0.8 %copy-start.4 = (bf16[128,128]{1,0:T(8,128)(2,1)S(1)}, bf16[128,128]{1,0:T(8,128)(2,1)}, u32[]{:S(2)}) copy-start(bf16[128,128]{1,0:T(8,128)(2,1)} %param.15) | copy-start | bytes 98308
  39.9 3.6 %copy-start.7 = (bf16[128,4]{0,1:T(4,128)(2,1)S(1)}, bf16[128,4]{0,1:T(4,128)(2,1)}, u32[]{:S(2)}) copy-start(bf16[128,4]{0,1:T(4,128)(2,1)} %param.17) | copy-start | bytes 3076
  39.9 10.4 %all-to-all-start.3 = ((bf16[16,2,3,256]{3,1,2,0:T(2,128)(2,1)}), bf16[16,2,3,256]{3,1,2,0:T(2,128)(2,1)S(1)}, u32[]{:S(2)}, u32[]{:S(2)}) async-start(bf16[16,2,3,256]{3,1,2,0:T(2,128)(2,1)} %reshape.157), calls=%async_computation.3 | async-start | bytes 98304 | tf_op jit(solution)/shard_map/all_to_all | solution.py:101
  50.9 10.0 %all-to-all-start.4 = ((f32[16,2,32]{2,1,0:T(2,128)}), f32[16,2,32]{2,1,0:T(2,128)S(1)}, u32[]{:S(2)}, u32[]{:S(2)}) async-start(f32[16,2,32]{2,1,0:T(2,128)} %bitcast.36), calls=%async_computation.4 | async-start | bytes 32768 | tf_op jit(solution)/shard_map/all_to_all | solution.py:103
  71.4 0.8 %copy-start.5 = (bf16[128,128]{1,0:T(8,128)(2,1)S(1)}, bf16[128,128]{1,0:T(8,128)(2,1)}, u32[]{:S(2)}) copy-start(bf16[128,128]{1,0:T(8,128)(2,1)} %param.19) | copy-start | bytes 98308
  71.4 0.8 %copy-start.6 = (bf16[128,128]{1,0:T(8,128)(2,1)S(1)}, bf16[128,128]{1,0:T(8,128)(2,1)}, u32[]{:S(2)}) copy-start(bf16[128,128]{1,0:T(8,128)(2,1)} %param.18) | copy-start | bytes 98308
where the time goes:
time: 73.7 us; the launch traced here: 73.1 us
  waiting for transfers between devices  30.6 us (42%)
  starting transfers between devices  21.7 us (29%)
  blocking collectives  9.07 us (12%)
  local copies, waits for them, and re-layouts  6.74 us (9%)
  matrix products  3.16 us (4%)
  other arithmetic  1.51 us (2%)
    all_to_all x1, blocking collectives, local(): lax.all_to_all(attended.reshape(residues, group_width, HEAD_DIM), 'rows',...  9.07 us
    all_to_all x1, starting transfers between devices, local(): lax.all_to_all(left_side, 'rows', split_axis=0, concat_axis=1, tiled=True)  7.41 us
    all_to_all x1, waiting for transfers between devices, local(): lax.all_to_all(outgoing, 'rows', split_axis=0, concat_axis=1, tiled=True)  6.51 us
    all_to_all x1, waiting for transfers between devices, local(): lax.all_to_all(product, 'rows', split_axis=1, concat_axis=0, tiled=True)  6.3 us
    all_to_all x1, waiting for transfers between devices, local(): lax.all_to_all(bias_copies, 'rows', split_axis=0, concat_axis=1, tiled=True)  6.08 us
    all_to_all x1, waiting for transfers between devices, local(): lax.all_to_all(right_side, 'rows', split_axis=0, concat_axis=1, tiled=True)  6.03 us
    all_to_all x1, waiting for transfers between devices, local(): lax.all_to_all(left_side, 'rows', split_axis=0, concat_axis=1, tiled=True)  5.67 us
    unnamed x27, local copies, waits for them, and re-layouts  4.13 us
  transfers between devices with their start and end apart: 5, of which 5 were waited for; matrix products, arithmetic and copies ran while one was open for 3% of the time, Pallas kernels for 0%

commit v1 on v0

v1 whole, which is shorter than its diff:
```python
import functools

import jax
import jax.numpy as jnp
from jax import lax
from jax.experimental import pallas as pl
from jax.experimental.pallas import tpu as pltpu
from jax.sharding import PartitionSpec as P

HEADS = 4
HEAD_DIM = 32
EPSILON = 1e-05
MASK_PENALTY = 1000000000.0
FAR = -1e30
MESH = pl.DeviceIdType.MESH
F32 = jnp.float32
BF16 = jnp.bfloat16
UNROLL = 4


def layer_norm(values):
    center = jnp.mean(values, axis=-1, keepdims=True)
    shifted = values - center
    spread = jnp.mean(shifted * shifted, axis=-1, keepdims=True)
    return shifted * lax.rsqrt(spread + EPSILON)


def dot(a, b):
    return lax.dot_general(a, b, (((1,), (0,)), ((), ())), preferred_element_type=F32)


def dot_nt(a, b):
    return lax.dot_general(a, b, (((1,), (1,)), ((), ())), preferred_element_type=F32)


def repeat(count, body):
    if count <= UNROLL:
        for step in range(count):
            body(step)
    else:
        lax.fori_loop(0, count, lambda step, carry: (body(step), carry)[1], 0)


def iota(shape, axis):
    return lax.broadcasted_iota(jnp.int32, shape, axis)


def kernel(
    n,
    pair_hbm, mask_ref, tri_in_hbm, tri_gate_hbm, tri_out_hbm, qkv_hbm, bias_hbm, gate_hbm, out_hbm,
    result_ref,
    pair_ref, tri_in, tri_gate, tri_out, qkv, att_bias, att_gate, att_out,
    right_buf, input_buf, product, attended,
    load_sem, send_sem, recv_sem,
):
    rows, residues, channels = pair_ref.shape
    total = rows * residues
    chips = n // 2
    me = lax.axis_index("rows")
    chip, core = me // 2, lax.rem(me, 2)
    partner = chip * 2 + (1 - core)

    def peer(offset):
        return lax.rem(chip + offset, chips) * 2 + core

    loads = [
        pltpu.make_async_copy(source, target, load_sem.at[k])
        for k, (source, target) in enumerate(
            [
                (pair_hbm, pair_ref), (tri_in_hbm, tri_in), (tri_gate_hbm, tri_gate),
                (tri_out_hbm, tri_out), (qkv_hbm, qkv), (bias_hbm, att_bias),
                (gate_hbm, att_gate), (out_hbm, att_out),
            ]
        )
    ]
    for load in loads:
        load.start()

    barrier = pltpu.get_barrier_semaphore()

    def greet(device):
        pl.semaphore_signal(barrier, inc=1, device_id={"rows": device}, device_id_type=MESH)

    greet(partner)
    for offset in range(1, chips):
        greet(peer(offset))

    def transfer(buf, which, source, device, slot):
        return pltpu.make_async_remote_copy(
            src_ref=buf.at[source],
            dst_ref=buf.at[source],
            send_sem=send_sem.at[which, slot],
            recv_sem=recv_sem.at[which, source],
            device_id={"rows": device},
            device_id_type=MESH,
        )

    def send_own(buf, which):
        for offset in range(1, chips):
            transfer(buf, which, me, peer(offset), offset).start()
        transfer(buf, which, me, partner, 0).start()

    def forward(buf, which):
        for offset in range(1, chips):
            source = peer(offset)
            transfer(buf, which, source, partner, 0).wait_recv()
            transfer(buf, which, source, partner, chips + offset).start()
        transfer(buf, which, partner, partner, 0).wait_recv()
        for offset in range(1, chips):
            source = lax.rem(chip + offset, chips) * 2 + (1 - core)
            transfer(buf, which, source, partner, 0).wait_recv()

    def finish(buf, which):
        transfer(buf, which, me, partner, 0).wait_send()
        for offset in range(1, chips):
            transfer(buf, which, me, partner, offset).wait_send()
            transfer(buf, which, me, partner, chips + offset).wait_send()

    loads[0].wait()
    first_row = me * rows
    pair = pair_ref[...].reshape(total, channels).astype(F32)
    normed = layer_norm(pair).astype(BF16)
    mask_row = mask_ref[...].astype(F32)
    lane = iota((total, residues), 1)
    line = iota((total, residues), 0)
    key_mask = jnp.sum(jnp.where(lane == line % residues, mask_row, 0.0), axis=1, keepdims=True)
    own_mask = jnp.sum(
        jnp.where(lane == line // residues + first_row, mask_row, 0.0), axis=1, keepdims=True
    )
    pair_mask = key_mask * own_mask
    loads[1].wait()

    def edge(side):
        start = side * 2 * channels
        both = dot(normed, tri_in[:, start : start + 2 * channels])
        return (jax.nn.sigmoid(both[:, :channels]) * both[:, channels:] * pair_mask).astype(BF16)

    right_buf[me] = edge(1).reshape(rows, residues, channels)
    pl.semaphore_wait(barrier, chips)
    send_own(right_buf, 0)
    left = edge(0).astype(F32).reshape(rows, residues, channels)
    loads[2].wait()
    triangle_gate = jax.nn.sigmoid(dot(normed, tri_gate[...]))
    for load in loads[3:]:
        load.wait()

    spread_rows = HEADS * 8
    head_pick = (iota((spread_rows, HEADS), 0) // 8 == iota((spread_rows, HEADS), 1)).astype(BF16)
    bias_rows = dot_nt(head_pick, att_bias[...]).astype(BF16)
    keys = residues * 8
    key_line = iota((residues, keys), 1) // 8 == iota((residues, keys), 0)
    penalty = jnp.sum(
        jnp.where(key_line, (key_mask[:residues] - 1.0) * MASK_PENALTY, 0.0), axis=0, keepdims=True
    )
    same_column = (iota((spread_rows, keys), 0) % 8) == (iota((spread_rows, keys), 1) % 8)
    penalty = jnp.where(same_column, penalty, FAR)

    forward(right_buf, 0)
    group = 8 // rows

    def contract(step):
        start = step * group
        block = right_buf[pl.ds(start, group)].astype(F32).reshape(8, residues, channels)
        at = step * 8 if isinstance(step, int) else pl.multiple_of(step * 8, 8)
        for i in range(rows):
            product[i, pl.ds(at, 8), :] = jnp.sum(block * left[i][None], axis=1)

    repeat(n // group, contract)
    triangle = product[...].reshape(total, channels).astype(BF16).astype(F32)
    triangle_normed = layer_norm(triangle).astype(BF16)
    update = dot(triangle_normed, tri_out[...])
    middle = (pair + triangle_gate * update).astype(BF16).astype(F32)
    attention_input = layer_norm(middle).astype(BF16)
    input_buf[me] = attention_input.reshape(rows, residues, channels)
    send_own(input_buf, 1)

    inner = HEADS * HEAD_DIM
    attention_gate = jax.nn.sigmoid(dot(attention_input, att_gate[...]))
    query = dot(attention_input, qkv[:, :inner]).astype(BF16).astype(F32)
    attended[...] = query.reshape(rows, residues, inner)
    head_of_lane = iota((8, inner), 1) // HEAD_DIM
    finish(right_buf, 0)
    forward(input_buf, 1)

    slab_start = pl.multiple_of(first_row // 16 * 16, 16)
    slab = input_buf[:, :, pl.ds(slab_start, 16), :].astype(F32).reshape(residues, 16, channels)
    within = iota((residues, 16, channels), 1)
    biases = []
    for i in range(rows):
        column = jnp.sum(
            jnp.where(within == first_row - slab_start + i, slab, 0.0), axis=1, keepdims=True
        )
        column = jnp.broadcast_to(column, (residues, 8, channels)).reshape(keys, channels)
        biases.append(dot_nt(bias_rows, column.astype(BF16)) + penalty)
    bias = jnp.concatenate(biases, axis=0)
    scale = HEAD_DIM ** (-0.5)

    def attend(step):
        at = step * 16 if isinstance(step, int) else pl.multiple_of(step * 16, 16)
        source = input_buf[:, :, pl.ds(at, 16), :].reshape(residues * 16, channels)
        both = dot(source, qkv[:, inner:]).reshape(residues, 16, 2 * inner)
        for half in range(2):
            piece = both[:, half * 8 : half * 8 + 8].reshape(keys, 2 * inner).astype(BF16)
            key, value = piece[:, :inner], piece[:, inner:]
            spot = at + half * 8
            if not isinstance(step, int):
                spot = pl.multiple_of(spot, 8)
            queries = []
            for i in range(rows):
                q = attended[i, pl.ds(spot, 8), :]
                queries += [jnp.where(head_of_lane == h, q, 0.0) for h in range(HEADS)]
            scores = dot_nt(jnp.concatenate(queries, axis=0).astype(BF16), key) * scale + bias
            peak = jnp.max(scores, axis=1, keepdims=True)
            weights = jnp.exp(scores - peak)
            weights = (weights / jnp.sum(weights, axis=1, keepdims=True)).astype(BF16)
            mixed = dot(weights, value)
            for i in range(rows):
                picked = jnp.zeros((8, inner), F32)
                for h in range(HEADS):
                    line = (i * HEADS + h) * 8
                    picked = jnp.where(head_of_lane == h, mixed[line : line + 8], picked)
                attended[i, pl.ds(spot, 8), :] = picked

    repeat(residues // 16, attend)
    heads = attended[...].reshape(total, inner).astype(BF16).astype(F32)
    gated = (attention_gate * heads).astype(BF16)
    final = middle + dot(gated, att_out[...])
    result_ref[...] = final.astype(BF16).reshape(rows, residues, channels)
    finish(input_buf, 1)


def solution(mesh):
    n = mesh.shape["rows"]

    def local(pair, mask, *weights):
        rows, residues, channels = pair.shape
        anywhere = pl.BlockSpec(memory_space=pl.ANY)
        vmem = pl.BlockSpec(memory_space=pltpu.VMEM)
        return pl.pallas_call(
            functools.partial(kernel, n),
            out_shape=jax.ShapeDtypeStruct(pair.shape, BF16),
            in_specs=[anywhere, vmem] + [anywhere] * len(weights),
            out_specs=vmem,
            scratch_shapes=[pltpu.VMEM(pair.shape, BF16)]
            + [pltpu.VMEM(w.shape, BF16) for w in weights]
            + [
                pltpu.VMEM((n,) + pair.shape, BF16),
                pltpu.VMEM((n,) + pair.shape, BF16),
                pltpu.VMEM(pair.shape, F32),
                pltpu.VMEM(pair.shape, F32),
                pltpu.SemaphoreType.DMA((1 + len(weights),)),
                pltpu.SemaphoreType.DMA((2, n)),
                pltpu.SemaphoreType.DMA((2, n)),
            ],
            compiler_params=pltpu.CompilerParams(
                collective_id=0, has_side_effects=True, vmem_limit_bytes=62 * 1024 * 1024
            ),
        )(pair, mask.reshape(1, -1), *weights)

    placed = (P(("parts", "rows"), None, None), P("parts")) + (P(),) * 7
    return jax.shard_map(
        local,
        mesh=mesh,
        in_specs=placed,
        out_specs=P(("parts", "rows"), None, None),
        check_vma=False,
    )
```

time: 73.7 us -> 24.2 us (0.33)
  waiting for transfers between devices: 30.6 us -> 0 us
  starting transfers between devices: 21.7 us -> 0 us
  Pallas kernels: 0 us -> 21 us
  blocking collectives: 9.07 us -> 0 us
  local copies, waits for them, and re-layouts: 6.74 us -> 2.74 us
  matrix products: 3.16 us -> 0 us
  other arithmetic: 1.51 us -> 0 us
    all_to_all x5 -> x0, waiting for transfers between devices: 30.6 us -> none  [the longest x1 6.51 us: local(): lax.all_to_all(outgoing, 'rows', split_axis=0, concat_axis=1, tiled=True)]
    all_to_all x5 -> x0, starting transfers between devices: 21.7 us -> none  [the longest x1 7.41 us: local(): lax.all_to_all(left_side, 'rows', split_axis=0, concat_axis=1, tiled=True)]
    pallas_call x0 -> x1, Pallas kernels: none -> 21 us  [local(): pl.pallas_call(functools.partial(kernel, n), out_shape=jax.ShapeDtypeStru...]
    all_to_all x1 -> x0, blocking collectives: 9.07 us -> none  [local(): lax.all_to_all(attended.reshape(residues, group_width, HEAD_DIM), 'rows',...]
    dot_general x11 -> x0, matrix products: 2.8 us -> none  [the longest x1 0.94 us: local(): jnp.einsum('rjf,fc->rjc', gated_output, w_att_out, preferred_element_type...]
    unnamed x27 -> x4, local copies, waits for them, and re-layouts: 4.13 us -> 2.74 us
    reshape x3 -> x0, local copies, waits for them, and re-layouts: 0.96 us -> none  [the longest x2 0.81 us: local(): projections.reshape(devices, row_count, 3, group_width * HEAD_DIM)]
    convert_element_type x4 -> x0, other arithmetic: 0.82 us -> none  [the longest x1 0.71 us: local(): key_mask = mask.astype(jnp.float32)]
  transfers between devices with their start and end apart: 5 -> 0, of which waited for: 5 -> 0; matrix products, arithmetic and copies ran while one was open for 3% -> 0% of each run, Pallas kernels for 0% -> 0%
where the time goes in v1:
time: 24.2 us; the launch traced here: 23.8 us
  Pallas kernels  21 us (87%)
  local copies, waits for them, and re-layouts  2.74 us (11%)
    pallas_call x1, Pallas kernels, local(): pl.pallas_call(functools.partial(kernel, n), out_shape=jax.ShapeDtypeStru...  21 us
    unnamed x4, local copies, waits for them, and re-layouts  2.74 us

profile of v1, /device:TPU:0, one launch (start us, length us, event | category | flops | bytes accessed | tf_op | source)
XLA Modules:
  0.0 23.8 jit_solution(18115060976624269409)
XLA Ops:
  0.0 0.0 copy-start
  0.0 0.7 %copy-done = bf16[128,4]{0,1:T(4,128)(2,1)S(1)} copy-done((bf16[128,4]{0,1:T(4,128)(2,1)S(1)}, bf16[128,4]{0,1:T(4,128)(2,1)}, u32[]{:S(2)}) %copy-start) | copy-done | bytes 1048
  0.7 0.7 %copy.10.bias_hbm = bf16[128,4]{1,0:T(8,128)(2,1)} copy(bf16[128,4]{0,1:T(4,128)(2,1)S(1)} %copy-done) | data formatting | bytes 2048 | tf_op args[6]
  1.4 21.0 %shard_map.91 = bf16[2,32,128]{2,1,0:T(8,128)(2,1)} custom-call(bf16[2,32,128]{2,1,0:T(8,128)(2,1)} %pair_hbm.1, s32[1,32]{1,0:T(1,128)} %bitcast.1, bf16[128,512]{1,0:T(8,128)(2,1)} %tri_in_hbm.1, bf16[128,128]{1,0:T(8,128)(2,1)} %tri_gate_hbm.1, bf16[128,128]{1,0:T(8,128)(2,1)} %tri_out_hbm.1, bf16[128,384]{1,0:T(8,128)(2,1)} %qkv_hbm.1, ...), custom_call_target="tpu_custom_call" | custom-call | tf_op jit(solution)/shard_map/pallas_call | solution.py:239
  22.5 1.3 %copy.12 = bf16[2,32,128]{2,1,0:T(8,128)(2,1)} copy(bf16[2,32,128]{2,1,0:T(8,128)(2,1)} %shard_map.91) | data formatting | bytes 32768
Async XLA Ops:
  0.0 0.7 %copy-start = (bf16[128,4]{0,1:T(4,128)(2,1)S(1)}, bf16[128,4]{0,1:T(4,128)(2,1)}, u32[]{:S(2)}) copy-start(bf16[128,4]{0,1:T(4,128)(2,1)} %param.15) | copy-start | bytes 3076

commit v2 on v1

--- a/solution.py
+++ b/solution.py
@@ -41,6 +41,12 @@
         lax.fori_loop(0, count, lambda step, carry: (body(step), carry)[1], 0)
 
 
+def split(n):
+    chips = n // 2
+    minor = 1 << ((chips.bit_length() - 1) // 2)
+    return chips, minor, chips // minor
+
+
 def iota(shape, axis):
     return lax.broadcasted_iota(jnp.int32, shape, axis)
 
@@ -50,18 +56,29 @@
     pair_hbm, mask_ref, tri_in_hbm, tri_gate_hbm, tri_out_hbm, qkv_hbm, bias_hbm, gate_hbm, out_hbm,
     result_ref,
     pair_ref, tri_in, tri_gate, tri_out, qkv, att_bias, att_gate, att_out,
-    right_buf, input_buf, product, attended,
+    right_buf, input_buf, product, attended, queries,
     load_sem, send_sem, recv_sem,
 ):
     rows, residues, channels = pair_ref.shape
     total = rows * residues
-    chips = n // 2
     me = lax.axis_index("rows")
+    chips, minor, major = split(n)
     chip, core = me // 2, lax.rem(me, 2)
+    place, spot_minor = chip // minor, lax.rem(chip, minor)
     partner = chip * 2 + (1 - core)
 
-    def peer(offset):
-        return lax.rem(chip + offset, chips) * 2 + core
+    def at_place(a, b, c):
+        return (a * minor + b) * 2 + c
+
+    def far(k):
+        up = k + (k - place + major) // major
+        down_raw = major - 1 - k
+        down = down_raw - (place - down_raw + major) // major
+        high = place // ((major + 1) // 2)
+        return high * up + (1 - high) * down
+
+    majors = [far(k) for k in range(major - 1)]
+    minors = [lax.rem(spot_minor + o, minor) for o in range(1, minor)]
 
     loads = [
         pltpu.make_async_copy(source, target, load_sem.at[k])
@@ -82,8 +99,13 @@
         pl.semaphore_signal(barrier, inc=1, device_id={"rows": device}, device_id_type=MESH)
 
     greet(partner)
-    for offset in range(1, chips):
-        greet(peer(offset))
+    for a in majors:
+        greet(at_place(a, spot_minor, core))
+    for b in minors:
+        greet(at_place(place, b, core))
+    for a in majors:
+        for b in minors:
+            greet(at_place(a, b, core))
 
     def transfer(buf, which, source, device, slot):
         return pltpu.make_async_remote_copy(
@@ -95,26 +117,45 @@
             device_id_type=MESH,
         )
 
+    def arrived(buf, which, source):
+        transfer(buf, which, source, partner, 0).wait_recv()
+
     def send_own(buf, which):
-        for offset in range(1, chips):
-            transfer(buf, which, me, peer(offset), offset).start()
+        slot = 1
+        for a in majors:
+            for b in minors + [spot_minor]:
+                transfer(buf, which, me, at_place(a, b, core), slot).start()
+                slot += 1
+        for b in minors:
+            transfer(buf, which, me, at_place(place, b, core), slot).start()
+            slot += 1
         transfer(buf, which, me, partner, 0).start()
 
     def forward(buf, which):
-        for offset in range(1, chips):
-            source = peer(offset)
-            transfer(buf, which, source, partner, 0).wait_recv()
-            transfer(buf, which, source, partner, chips + offset).start()
-        transfer(buf, which, partner, partner, 0).wait_recv()
-        for offset in range(1, chips):
-            source = lax.rem(chip + offset, chips) * 2 + (1 - core)
-            transfer(buf, which, source, partner, 0).wait_recv()
+        slot = chips
+        def to_partner(source):
+            nonlocal slot
+            transfer(buf, which, source, partner, slot).start()
+            slot += 1
+        for b in minors:
+            source = at_place(place, b, core)
+            arrived(buf, which, source)
+            to_partner(source)
+        for a in reversed(majors):
+            for b in [spot_minor] + minors:
+                source = at_place(a, b, core)
+                arrived(buf, which, source)
+                to_partner(source)
+        arrived(buf, which, partner)
+        for b in minors:
+            arrived(buf, which, at_place(place, b, 1 - core))
+        for a in reversed(majors):
+            for b in [spot_minor] + minors:
+                arrived(buf, which, at_place(a, b, 1 - core))
 
     def finish(buf, which):
-        transfer(buf, which, me, partner, 0).wait_send()
-        for offset in range(1, chips):
-            transfer(buf, which, me, partner, offset).wait_send()
-            transfer(buf, which, me, partner, chips + offset).wait_send()
+        for slot in range(2 * chips - 1):
+            transfer(buf, which, me, partner, slot).wait_send()
 
     loads[0].wait()
     first_row = me * rows
@@ -144,15 +185,16 @@
     for load in loads[3:]:
         load.wait()
 
-    spread_rows = HEADS * 8
-    head_pick = (iota((spread_rows, HEADS), 0) // 8 == iota((spread_rows, HEADS), 1)).astype(BF16)
-    bias_rows = dot_nt(head_pick, att_bias[...]).astype(BF16)
-    keys = residues * 8
-    key_line = iota((residues, keys), 1) // 8 == iota((residues, keys), 0)
+    width = 16
+    spread_rows = HEADS * width
+    head_pick = (iota((spread_rows, HEADS), 0) // width == iota((spread_rows, HEADS), 1)).astype(BF16)
+    bias_rows = dot(head_pick, att_bias[...]).astype(BF16)
+    keys = residues * width
+    key_line = iota((residues, keys), 1) // width == iota((residues, keys), 0)
     penalty = jnp.sum(
         jnp.where(key_line, (key_mask[:residues] - 1.0) * MASK_PENALTY, 0.0), axis=0, keepdims=True
     )
-    same_column = (iota((spread_rows, keys), 0) % 8) == (iota((spread_rows, keys), 1) % 8)
+    same_column = (iota((spread_rows, keys), 0) % width) == (iota((spread_rows, keys), 1) % width)
     penalty = jnp.where(same_column, penalty, FAR)
 
     forward(right_buf, 0)
@@ -177,51 +219,49 @@
     inner = HEADS * HEAD_DIM
     attention_gate = jax.nn.sigmoid(dot(attention_input, att_gate[...]))
     query = dot(attention_input, qkv[:, :inner]).astype(BF16).astype(F32)
-    attended[...] = query.reshape(rows, residues, inner)
-    head_of_lane = iota((8, inner), 1) // HEAD_DIM
+    query = query.reshape(rows, residues, inner)
+    head_of_lane = iota((width, inner), 1) // HEAD_DIM
+    scale = HEAD_DIM ** (-0.5)
+    per_block = rows * spread_rows
+    for block in range(residues // width):
+        parts = []
+        for i in range(rows):
+            q = query[i, block * width : (block + 1) * width]
+            parts += [jnp.where(head_of_lane == h, q, 0.0) for h in range(HEADS)]
+        turned = dot_nt(jnp.concatenate(parts, axis=0).astype(BF16), qkv[:, inner : 2 * inner])
+        queries[block] = (turned * scale).astype(BF16)
     finish(right_buf, 0)
     forward(input_buf, 1)
 
-    slab_start = pl.multiple_of(first_row // 16 * 16, 16)
-    slab = input_buf[:, :, pl.ds(slab_start, 16), :].astype(F32).reshape(residues, 16, channels)
-    within = iota((residues, 16, channels), 1)
+    slab_start = pl.multiple_of(first_row // width * width, width)
+    slab = input_buf[:, :, pl.ds(slab_start, width), :].astype(F32).reshape(residues, width, channels)
+    within = iota((residues, width, channels), 1)
     biases = []
     for i in range(rows):
         column = jnp.sum(
             jnp.where(within == first_row - slab_start + i, slab, 0.0), axis=1, keepdims=True
         )
-        column = jnp.broadcast_to(column, (residues, 8, channels)).reshape(keys, channels)
+        column = jnp.broadcast_to(column, (residues, width, channels)).reshape(keys, channels)
         biases.append(dot_nt(bias_rows, column.astype(BF16)) + penalty)
     bias = jnp.concatenate(biases, axis=0)
-    scale = HEAD_DIM ** (-0.5)
 
     def attend(step):
-        at = step * 16 if isinstance(step, int) else pl.multiple_of(step * 16, 16)
-        source = input_buf[:, :, pl.ds(at, 16), :].reshape(residues * 16, channels)
-        both = dot(source, qkv[:, inner:]).reshape(residues, 16, 2 * inner)
-        for half in range(2):
-            piece = both[:, half * 8 : half * 8 + 8].reshape(keys, 2 * inner).astype(BF16)
-            key, value = piece[:, :inner], piece[:, inner:]
-            spot = at + half * 8
-            if not isinstance(step, int):
-                spot = pl.multiple_of(spot, 8)
-            queries = []
-            for i in range(rows):
-                q = attended[i, pl.ds(spot, 8), :]
-                queries += [jnp.where(head_of_lane == h, q, 0.0) for h in range(HEADS)]
-            scores = dot_nt(jnp.concatenate(queries, axis=0).astype(BF16), key) * scale + bias
-            peak = jnp.max(scores, axis=1, keepdims=True)
-            weights = jnp.exp(scores - peak)
-            weights = (weights / jnp.sum(weights, axis=1, keepdims=True)).astype(BF16)
-            mixed = dot(weights, value)
-            for i in range(rows):
-                picked = jnp.zeros((8, inner), F32)
-                for h in range(HEADS):
-                    line = (i * HEADS + h) * 8
-                    picked = jnp.where(head_of_lane == h, mixed[line : line + 8], picked)
-                attended[i, pl.ds(spot, 8), :] = picked
-
-    repeat(residues // 16, attend)
+        at = step * width if isinstance(step, int) else pl.multiple_of(step * width, width)
+        source = input_buf[:, :, pl.ds(at, width), :].reshape(keys, channels)
+        scores = dot_nt(queries[step], source) + bias
+        peak = jnp.max(scores, axis=1, keepdims=True)
+        weights = jnp.exp(scores - peak)
+        whole = jnp.sum(weights, axis=1, keepdims=True)
+        mixed = dot(weights.astype(BF16), source) / whole
+        valued = dot(mixed.astype(BF16), qkv[:, 2 * inner :])
+        for i in range(rows):
+            picked = jnp.zeros((width, inner), F32)
+            for h in range(HEADS):
+                line = (i * HEADS + h) * width
+                picked = jnp.where(head_of_lane == h, valued[line : line + width], picked)
+            attended[i, pl.ds(at, width), :] = picked
+
+    repeat(residues // width, attend)
     heads = attended[...].reshape(total, inner).astype(BF16).astype(F32)
     gated = (attention_gate * heads).astype(BF16)
     final = middle + dot(gated, att_out[...])
@@ -233,6 +273,7 @@
     n = mesh.shape["rows"]
 
     def local(pair, mask, *weights):
+        weights = weights[:4] + (weights[4].T,) + weights[5:]
         rows, residues, channels = pair.shape
         anywhere = pl.BlockSpec(memory_space=pl.ANY)
         vmem = pl.BlockSpec(memory_space=pltpu.VMEM)
@@ -248,12 +289,13 @@
                 pltpu.VMEM((n,) + pair.shape, BF16),
                 pltpu.VMEM(pair.shape, F32),
                 pltpu.VMEM(pair.shape, F32),
+                pltpu.VMEM((residues // 16, rows * HEADS * 16, HEADS * HEAD_DIM), BF16),
                 pltpu.SemaphoreType.DMA((1 + len(weights),)),
                 pltpu.SemaphoreType.DMA((2, n)),
                 pltpu.SemaphoreType.DMA((2, n)),
             ],
             compiler_params=pltpu.CompilerParams(
-                collective_id=0, has_side_effects=True, vmem_limit_bytes=62 * 1024 * 1024
+                collective_id=0, has_side_effects=True, vmem_limit_bytes=62 << 20
             ),
         )(pair, mask.reshape(1, -1), *weights)
 

time: 24.2 us -> 21.8 us (0.901)
  local copies, waits for them, and re-layouts: 2.74 us -> 1.32 us
  Pallas kernels: 21 us -> 20.1 us
    unnamed x4 -> x1, local copies, waits for them, and re-layouts: 2.74 us -> 1.32 us
    pallas_call x1, Pallas kernels: 21 us -> 20.1 us  [local(): pl.pallas_call(functools.partial(kernel, n), out_shape=jax.ShapeDtypeStru...]
where the time goes in v2:
time: 21.8 us; the launch traced here: 21.4 us
  Pallas kernels  20.1 us (92%)
  local copies, waits for them, and re-layouts  1.32 us (6%)
    pallas_call x1, Pallas kernels, local(): pl.pallas_call(functools.partial(kernel, n), out_shape=jax.ShapeDtypeStru...  20.1 us
    unnamed x1, local copies, waits for them, and re-layouts  1.32 us

profile of v2, /device:TPU:0, one launch (start us, length us, event | category | flops | bytes accessed | tf_op | source)
XLA Modules:
  0.0 21.4 jit_solution(15998465494324139131)
XLA Ops:
  0.0 20.1 %shard_map.91 = bf16[2,32,128]{2,1,0:T(8,128)(2,1)} custom-call(bf16[2,32,128]{2,1,0:T(8,128)(2,1)} %pair_hbm.1, s32[1,32]{1,0:T(1,128)} %bitcast.3, bf16[128,512]{1,0:T(8,128)(2,1)} %tri_in_hbm.1, bf16[128,128]{1,0:T(8,128)(2,1)} %tri_gate_hbm.1, bf16[128,128]{1,0:T(8,128)(2,1)} %tri_out_hbm.1, bf16[128,384]{1,0:T(8,128)(2,1)} %qkv_hbm.1, ...), custom_call_target="tpu_custom_call" | custom-call | tf_op jit(solution)/shard_map/pallas_call | solution.py:280
  20.1 1.3 %copy.11 = bf16[2,32,128]{2,1,0:T(8,128)(2,1)} copy(bf16[2,32,128]{2,1,0:T(8,128)(2,1)} %shard_map.91) | data formatting | bytes 32768

commit v3 on v2

--- a/solution.py
+++ b/solution.py
@@ -16,6 +16,7 @@
 F32 = jnp.float32
 BF16 = jnp.bfloat16
 UNROLL = 4
+VMEM_LIMIT = int(53.905 * 2**20)
 
 
 def layer_norm(values):
@@ -90,8 +91,7 @@
             ]
         )
     ]
-    for load in loads:
-        load.start()
+    loads[0].start()
 
     barrier = pltpu.get_barrier_semaphore()
 
@@ -106,6 +106,9 @@
     for a in majors:
         for b in minors:
             greet(at_place(a, b, core))
+
+    for load in loads[1:]:
+        load.start()
 
     def transfer(buf, which, source, device, slot):
         return pltpu.make_async_remote_copy(
@@ -122,10 +125,10 @@
 
     def send_own(buf, which):
         slot = 1
-        for a in majors:
-            for b in minors + [spot_minor]:
-                transfer(buf, which, me, at_place(a, b, core), slot).start()
-                slot += 1
+        pairs = [(a, b) for b in minors for a in majors] + [(a, spot_minor) for a in majors]
+        for a, b in pairs:
+            transfer(buf, which, me, at_place(a, b, core), slot).start()
+            slot += 1
         for b in minors:
             transfer(buf, which, me, at_place(place, b, core), slot).start()
             slot += 1
@@ -295,7 +298,7 @@
                 pltpu.SemaphoreType.DMA((2, n)),
             ],
             compiler_params=pltpu.CompilerParams(
-                collective_id=0, has_side_effects=True, vmem_limit_bytes=62 << 20
+                collective_id=0, has_side_effects=True, vmem_limit_bytes=VMEM_LIMIT
             ),
         )(pair, mask.reshape(1, -1), *weights)
 

time: 21.8 us -> 20.2 us (0.927)
  Pallas kernels: 20.1 us -> 18.6 us
    pallas_call x1, Pallas kernels: 20.1 us -> 18.6 us  [local(): pl.pallas_call(functools.partial(kernel, n), out_shape=jax.ShapeDtypeStru...]
    unnamed x1 -> x5, local copies, waits for them, and re-layouts: 1.32 us -> 1.29 us
where the time goes in v3:
time: 20.2 us; the launch traced here: 19.9 us
  Pallas kernels  18.6 us (92%)
  local copies, waits for them, and re-layouts  1.29 us (6%)
    pallas_call x1, Pallas kernels, local(): pl.pallas_call(functools.partial(kernel, n), out_shape=jax.ShapeDtypeStru...  18.6 us
    unnamed x5, local copies, waits for them, and re-layouts  1.29 us

profile of v3, /device:TPU:0, one launch (start us, length us, event | category | flops | bytes accessed | tf_op | source)
XLA Modules:
  0.0 19.9 jit_solution(7300216124563345594)
XLA Ops:
  0.0 0.0 copy-start
  0.0 0.0 copy-start.1
  0.0 0.7 %copy-done = bf16[128,4]{0,1:T(4,128)(2,1)S(1)} copy-done((bf16[128,4]{0,1:T(4,128)(2,1)S(1)}, bf16[128,4]{0,1:T(4,128)(2,1)}, u32[]{:S(2)}) %copy-start) | copy-done | bytes 1048
  0.7 0.0 copy-done.1
  0.7 18.6 %shard_map.91 = bf16[2,32,128]{2,1,0:T(8,128)(2,1)S(1)} custom-call(bf16[2,32,128]{2,1,0:T(8,128)(2,1)} %pair_hbm.1, s32[1,32]{1,0:T(1,128)S(1)} %bitcast.3, bf16[128,512]{1,0:T(8,128)(2,1)} %tri_in_hbm.1, bf16[128,128]{1,0:T(8,128)(2,1)} %tri_gate_hbm.1, bf16[128,128]{1,0:T(8,128)(2,1)} %tri_out_hbm.1, bf16[128,384]{1,0:T(8,128)(2,1)} %qkv_hbm.1, ...), custom_call_target="tpu_custom_call" | custom-call | tf_op jit(solution)/shard_map/pallas_call | solution.py:283
  19.3 0.6 %copy.11 = bf16[2,32,128]{2,1,0:T(8,128)(2,1)} copy(bf16[2,32,128]{2,1,0:T(8,128)(2,1)S(1)} %shard_map.91) | data formatting | bytes 32768
Async XLA Ops:
  0.0 0.7 %copy-start = (bf16[128,4]{0,1:T(4,128)(2,1)S(1)}, bf16[128,4]{0,1:T(4,128)(2,1)}, u32[]{:S(2)}) copy-start(bf16[128,4]{0,1:T(4,128)(2,1)} %param.15) | copy-start | bytes 3076
  0.0 0.7 %copy-start.1 = (s32[32]{0:T(128)S(1)}, s32[32]{0:T(128)}, u32[]{:S(2)}) copy-start(s32[32]{0:T(128)} %param.10) | copy-start | bytes 388
